TPU v7x, 16 devices: a 4x2x1 block of a 4x4x8 slice. The times are simulated.
16 devices in a mesh: dp: 2 (over y, z), pp: 8 (over x, core).
Axes of the slice: x: 4, y: 2, z: 1, core: 2. Of those that a mesh axis runs over, the one named last changes fastest.
The devices are a block of a 4x4x8 slice.
Arguments:
- x_in: bfloat16 [16, 4, 128, 768], P(('dp', 'pp')), parts along dimension 0
- dy_out: bfloat16 [16, 4, 128, 768], P(('dp', 'pp')), parts along dimension 0
- w_qkv: bfloat16 [8, 2, 1, 768, 3, 16, 48], P('pp')
- w_attn: bfloat16 [8, 2, 1, 16, 48, 768], P('pp')
- w_fc: bfloat16 [8, 2, 1, 768, 3072], P('pp')
- w_proj: bfloat16 [8, 2, 1, 3072, 768], P('pp')
- b_qkv: bfloat16 [8, 2, 1, 3, 16, 48], P('pp')
- b_fc: bfloat16 [8, 2, 1, 3072], P('pp')
- vec_d: bfloat16 [8, 2, 1, 6, 768], P('pp')
Outputs:
- output 1: bfloat16 [16, 4, 128, 768], P(('dp', 'pp')), parts along dimension 0
- output 2: bfloat16 [16, 4, 128, 768], P(('dp', 'pp')), parts along dimension 0
- output 3: float32 [16, 2, 1, 768, 3, 16, 48], P(('dp', 'pp')), parts along dimension 0
- output 4: float32 [16, 2, 1, 16, 48, 768], P(('dp', 'pp')), parts along dimension 0
- output 5: float32 [16, 2, 1, 768, 3072], P(('dp', 'pp')), parts along dimension 0
- output 6: float32 [16, 2, 1, 3072, 768], P(('dp', 'pp')), parts along dimension 0
- output 7: float32 [16, 2, 1, 3, 16, 48], P(('dp', 'pp')), parts along dimension 0
- output 8: float32 [16, 2, 1, 3072], P(('dp', 'pp')), parts along dimension 0
- output 9: float32 [16, 2, 1, 6, 768], P(('dp', 'pp')), parts along dimension 0
There are 2 independent parts. A program takes and returns all parts, laid end to end along the dimension named above; an argument that names none is the same for every part.
All inputs are finite; a program needn't handle non-finite values.
Results may differ from a plain program's by a relative error of at most 0.02.
Values are sent between devices in bfloat16 or wider.
A program may use at most 768 MiB of HBM per device.

v0:
```python
import functools

import jax
import jax.numpy as jnp
from jax import lax
from jax.experimental import pallas as pl
from jax.experimental.pallas import tpu as pltpu
from jax.sharding import PartitionSpec as P

EPS = 1e-5
F32 = jnp.float32
BF16 = jnp.bfloat16
LANES = 128
ROWS = 96
CH = 256
SKEW = 8
K0 = 0.7978845608028654
K1 = K0 * 0.044715
VMEM_LIMIT = 67043328
HBM = pl.BlockSpec(memory_space=pl.ANY)


def dot(lhs, rhs, lc=1, rc=0):
    return lax.dot_general(lhs, rhs, (((lc,), (rc,)), ((), ())), preferred_element_type=F32)


def rows_sum(v):
    r, t = v.shape
    return jnp.sum(v.reshape(r // 8, 8, t), axis=0)


def column(cols, lane, row, count):
    return cols[row:row + count, lane:lane + 1].astype(F32)


def lane_fold(v):
    return functools.reduce(jnp.add, [v[:, k:k + LANES] for k in range(0, v.shape[1], LANES)])


def rounded(v):
    return v.astype(BF16).astype(F32)


def token_sum(v):
    return rounded(jnp.sum(lane_fold(v), axis=1, keepdims=True))


def block_diag(a, b):
    z = jnp.zeros_like(a)
    return jnp.concatenate([jnp.concatenate([a, z], 1), jnp.concatenate([z, b], 1)], 0)


def f_norm(src, cols, lane, dst, stats, row, hold):
    d, t = src.shape
    acc = jnp.zeros((8, t), F32)
    for i in range(0, d, ROWS):
        acc += rows_sum(src[i:i + ROWS, :].astype(F32))
    mean = jnp.sum(acc, axis=0, keepdims=True) * (1.0 / d)
    acc = jnp.zeros((8, t), F32)
    for i in range(0, d, ROWS):
        c = src[i:i + ROWS, :].astype(F32) - mean
        hold[i:i + ROWS, :] = c
        acc += rows_sum(c * c)
    rstd = lax.rsqrt(jnp.sum(acc, axis=0, keepdims=True) * (1.0 / d) + EPS)
    for i in range(0, d, ROWS):
        c = hold[i:i + ROWS, :] * rstd
        dst[i:i + ROWS, :] = (c * column(cols, lane, i, ROWS) + column(cols, lane + 1, i, ROWS)).astype(BF16)
    stats[row:row + 1, :] = mean
    stats[row + 1:row + 2, :] = rstd


def token_totals(v):
    return dot(v, jnp.ones((v.shape[1], LANES), BF16))


def b_norm(dn, src, cols, gain, skip, dst, stats, row, acc, lane, hold):
    d, t = src.shape
    mean = stats[row:row + 1, :]
    rstd = stats[row + 1:row + 2, :]
    at = lax.broadcasted_iota(jnp.int32, (ROWS, LANES), 1)
    m1 = dot(cols[...], dn[...], 0, 0)[gain:gain + 1, :] * (1.0 / d)
    shift = token_totals(dn[...])
    s2 = jnp.zeros((8, t), F32)
    for i in range(0, d, ROWS):
        c = (src[i:i + ROWS, :].astype(F32) - mean) * rstd
        hold[i:i + ROWS, :] = c
        w = dn[i:i + ROWS, :].astype(F32) * c
        s2 += rows_sum(w * column(cols, gain, i, ROWS))
        acc[i:i + ROWS, :] += jnp.where(at == lane, token_sum(w), jnp.where(at == lane + 1, rounded(shift[i:i + ROWS]), 0.0))
    m2 = jnp.sum(s2, axis=0, keepdims=True) * (1.0 / d)
    for i in range(0, d, ROWS):
        g = dn[i:i + ROWS, :].astype(F32) * column(cols, gain, i, ROWS)
        z = (g - m1 - hold[i:i + ROWS, :] * m2) * rstd + skip[i:i + ROWS, :].astype(F32)
        dst[i:i + ROWS, :] = z.astype(BF16)


def skewed(jobs, first, second):
    pending = []
    for job in jobs:
        pending.append((job, first(*job)))
        if len(pending) > SKEW:
            job, v = pending.pop(0)
            second(*job, v)
    for job, v in pending:
        second(*job, v)


def f_heads(t, o, p, heads, seq, after):
    d, n = o.shape
    head = d // heads
    two = 2 * head
    pairs = heads // 2
    key = lax.broadcasted_iota(jnp.int32, (seq, 2 * seq), 0)
    qry = lax.rem(lax.broadcasted_iota(jnp.int32, (seq, 2 * seq), 1), seq)
    ok = key <= qry
    c = (head ** -0.5) * 1.4426950408889634

    def score(b, j):
        r0, lanes = two * j, slice(b * seq, (b + 1) * seq)
        q = t[r0:r0 + two, lanes]
        return dot(t[d + r0:d + r0 + two, lanes], block_diag(q[:head], q[head:]), 0, 0)

    def mix(b, j, s):
        r0, lanes = two * j, slice(b * seq, (b + 1) * seq)
        s = jnp.where(ok, s, -1e30)
        m = jnp.max(s, axis=0, keepdims=True)
        e = jnp.exp2((s - m) * c)
        e = e * (1.0 / jnp.sum(e, axis=0, keepdims=True))
        k0 = (b * pairs + j) * seq
        p[k0:k0 + seq, :] = e
        x = dot(t[2 * d + r0:2 * d + r0 + two, lanes], e.astype(BF16))
        o[r0:r0 + head, lanes] = x[:head, :seq].astype(BF16)
        o[r0 + head:r0 + two, lanes] = x[head:, seq:].astype(BF16)
        if j == pairs - 1:
            after(b)

    skewed([(b, j) for b in range(n // seq) for j in range(pairs)], score, mix)


def b_heads(t, do, p, heads, seq, after):
    d, n = do.shape
    head = d // heads
    two = 2 * head
    pairs = heads // 2
    scale = head ** -0.5

    def first(b, j):
        r0, lanes = two * j, slice(b * seq, (b + 1) * seq)
        z = do[r0:r0 + two, lanes]
        return dot(t[2 * d + r0:2 * d + r0 + two, lanes], block_diag(z[:head], z[head:]), 0, 0)

    def diag(r0, lanes, x, k):
        t[r0:r0 + head, lanes] = (x[:head, :seq] * k).astype(BF16)
        t[r0 + head:r0 + two, lanes] = (x[head:, seq:] * k).astype(BF16)

    def second(b, j, dp):
        r0, lanes = two * j, slice(b * seq, (b + 1) * seq)
        k0 = (b * pairs + j) * seq
        e = p[k0:k0 + seq, :]
        w = e * dp
        ds = (w - e * jnp.sum(w, axis=0, keepdims=True)).astype(BF16)
        eb = e.astype(BF16)
        q, k = t[r0:r0 + two, lanes], t[d + r0:d + r0 + two, lanes]
        tall = jnp.concatenate([ds[:, :seq], ds[:, seq:]], 0)
        dq, dk = dot(k, ds), dot(q, tall, 1, 1)
        tall = jnp.concatenate([eb[:, :seq], eb[:, seq:]], 0)
        dv = dot(do[r0:r0 + two, lanes], tall, 1, 1)
        diag(r0, lanes, dq, scale)
        diag(d + r0, lanes, dk, scale)
        diag(2 * d + r0, lanes, dv, 1.0)
        if j == pairs - 1:
            after(b)

    skewed([(b, j) for b in range(n // seq) for j in range(pairs)], first, second)


def gelu_and_slope(x):
    x2 = x * x
    hp = 0.5 * jnp.tanh(x * (x2 * K1 + K0)) + 0.5
    u = x * hp
    return u, hp + (u - u * hp) * (x2 * (6.0 * K1) + 2.0 * K0)


ORDERS = (
    (0, 1, 2, 3, 4, 5, 6, 7, 8, 16, 9, 17, 10, 18, 11, 19, 12, 20, 13, 21, 14, 22, 15, 23, 24, 25, 26, 27, 28, 29, 30, 31),
    (0, 1, 2, 3, 4, 5, 6, 7, 8, 9, 16, 10, 17, 11, 12, 18, 13, 19, 14, 20, 15, 21, 24, 22, 25, 23, 26, 27, 28, 29, 30, 31),
    (0, 1, 2, 3, 8, 4, 9, 5, 10, 6, 11, 7, 12, 16, 13, 17, 14, 18, 15, 19, 24, 20, 25, 21, 26, 22, 27, 23, 28, 29, 30, 31),
    (0, 8, 1, 9, 2, 10, 3, 11, 4, 12, 5, 13, 6, 14, 7, 15, 16, 24, 17, 25, 18, 26, 19, 27, 20, 28, 21, 29, 22, 30, 23, 31),
)


class Group:
    def __init__(self, n):
        self.n, self.half, self.last, self.steps = n, n // 2, n - 1, 4 * n
        self.me = lax.axis_index('pp')
        self.side = self.me // self.half
        self.depth = self.me + self.side * (self.last - 2 * self.me)
        self.inner = self.me + 1 - 2 * self.side
        self.outer = self.me - 1 + 2 * self.side
        self.inside = self.depth == self.half - 1
        self.outside = self.depth == 0
        self.codes = []
        for k in range(self.steps):
            v = jnp.int32(ORDERS[0][k])
            for i in range(1, self.half):
                v = jnp.where(self.depth == i, ORDERS[i][k], v)
            self.codes.append(v)

    def place(self, i):
        far = lax.rem(i - self.half + self.half // 2, self.half) + self.half
        return jnp.where(i < self.half, i, far)

    def step(self, s):
        code = self.codes[0]
        for k in range(1, self.steps):
            code = jnp.where(s == k, self.codes[k], code)
        kind = code // self.n
        m = code - self.n * kind
        back = kind >= 2
        sec = jnp.where(jnp.logical_or(kind == 1, kind == 2), 1, 0)
        c = jnp.where(sec == 1, 1 - self.side, self.side)
        return kind, back, sec, m, c


def both(a, *rest):
    return functools.reduce(jnp.logical_and, rest, a)


def walk_kernel(n, heads, seq, x_in, dy_in, wq, wo, w1, w2, vec, bq, b1,
                y_out, dx_out, hs, ts, rs, ps, gs, ss, as_, os_, bs, us, dys, dgs, drs, dts, feed, sums, x_t, dy_t,
                vwq, vwo, vw1, vw2, vcols, vvec, vbq, vb1, slots, out, a, t, o, r, u, pg, ya, stats, acc,
                load_sems, recv_sems, send_sems, final_sems, feed_send, feed_recv, f_sems, b_in, b_sems, lead_sems):
    g = Group(n)
    d, tok = a.shape
    f = u.shape[0]
    half = tok // 2
    prow = ps.shape[2]
    part = prow // (tok // seq)
    weights = ((wq, vwq), (wo, vwo), (w1, vw1), (w2, vw2))

    def weight(c, i):
        h, v = weights[i]
        return pltpu.make_async_copy(h.at[c], v.at[c], load_sems.at[c, i])

    def remote(src, dst, send, recv, dev):
        return pltpu.make_async_remote_copy(src_ref=src, dst_ref=dst, send_sem=send, recv_sem=recv, device_id={'pp': dev})

    def saver(c, m, sems):
        def copy(i, v, dst, at=None):
            hbm = dst.at[c, m]
            if at is not None:
                v, hbm = v.at[pl.ds(*at), :], hbm.at[pl.ds(*at), :]
            return pltpu.make_async_copy(v, hbm, sems.at[i])
        return copy

    def fetch(i, c, m, at=None):
        hbm, v = ((gs, pg), (ps, pg.at[pl.ds(0, prow), :]), (ts, t), (rs, r), (hs, a), (ss, stats))[i]
        hbm = hbm.at[c, m]
        if at is not None:
            hbm, v = hbm.at[pl.ds(*at), :], v.at[pl.ds(*at), :]
        return pltpu.make_async_copy(hbm, v, b_in.at[i])

    def forward(c, m, x, y):
        copy = saver(c, m, f_sems)
        cv = vcols.at[c]
        copy(0, x, hs).start()
        f_norm(x, cv, 0, a, stats, 0, ya)
        copy(1, a, as_).start()
        v = a[...]
        for i in range(0, 3 * d, CH):
            z = dot(vwq[c, i:i + CH, :], v) + column(cv, 6 + i // d, i % d, CH)
            t[i:i + CH, :] = z.astype(BF16)
        copy(2, t, ts).start()
        f_heads(t, o, pg, heads, seq, lambda b: copy(4, pg, ps, (b * part, part)).start())
        copy(3, o, os_).start()
        v = o[...]
        for i in range(0, d, CH):
            z = dot(vwo[c, :, i:i + CH], v, 0, 0) + column(cv, 2, i, CH) + x[i:i + CH, :].astype(F32)
            r[i:i + CH, :] = z.astype(BF16)
        copy(5, r, rs).start()
        copy(1, a, as_).wait()
        f_norm(r, cv, 3, a, stats, 2, ya)
        copy(6, a, bs).start()
        copy(7, stats, ss).start()
        copy(4, pg.at[pl.ds(0, prow), :], ps).wait()
        v = a[...]

        def up(k):
            for i in range(k * d, (k + 1) * d, CH):
                h = dot(vw1[c, :, i:i + CH], v, 0, 0) + column(cv, 9 + k, i % d, CH)
                uu, slope = gelu_and_slope(h)
                u[i:i + CH, :] = uu.astype(BF16)
                pg[2 * i:2 * i + CH, :] = slope[:, :half]
                pg[2 * i + CH:2 * i + 2 * CH, :] = slope[:, half:]
                copy(8, u, us, (i, CH)).start()
                copy(9, pg, gs, (2 * i, 2 * CH)).start()

        def down(k):
            w = u[k * d:(k + 1) * d, :]
            for i in range(0, d, CH):
                z = dot(vw2[c, k * d:(k + 1) * d, i:i + CH], w, 0, 0)
                z += (column(cv, 5, i, CH) + r[i:i + CH, :].astype(F32)) if k == 0 else ya[i:i + CH, :]
                if (k + 1) * d < f:
                    ya[i:i + CH, :] = z
                else:
                    y[i:i + CH, :] = z.astype(BF16)

        up(0)
        for k in range(1, f // d):
            up(k)
            down(k - 1)
        down(f // d - 1)
        for i, v, dst in ((0, x, hs), (2, t, ts), (3, o, os_), (5, r, rs), (6, a, bs), (7, stats, ss), (8, u, us),
                          (9, pg, gs)):
            copy(i, v, dst).wait()

    def backward(c, m, dy, y, then):
        copy = saver(c, m, b_sems)
        cv = vcols.at[c]
        copy(0, dy, dys).start()
        fetch(0, c, m).wait()
        v = dy[...]
        for i in range(0, f, CH):
            du = dot(vw2[c, i:i + CH, :], v).astype(BF16).astype(F32)
            u[i:i + CH, :half] = (du[:, :half] * pg[2 * i:2 * i + CH, :]).astype(BF16)
            u[i:i + CH, half:] = (du[:, half:] * pg[2 * i + CH:2 * i + 2 * CH, :]).astype(BF16)
        fetch(1, c, m).start()
        then(0, (prow, 2 * f - prow))
        copy(1, u, dgs).start()
        v = u[...]
        for i in range(0, d, CH):
            y[i:i + CH, :] = dot(vw1[c, i:i + CH, :], v).astype(BF16)
        for i in (3, 4, 5):
            fetch(i, c, m).wait()
        b_norm(y, r, cv, 3, dy, o, stats, 2, acc.at[c], 2, ya)
        then(3)
        copy(2, o, drs).start()
        v = o[...]
        for i in range(0, d, CH):
            y[i:i + CH, :] = dot(vwo[c, i:i + CH, :], v).astype(BF16)
        for i in (1, 2):
            fetch(i, c, m).wait()
        b_heads(t, y, pg, heads, seq, lambda b: then(0, (b * part, part)))
        copy(3, t, dts).start()
        v = t[...]
        at = lax.broadcasted_iota(jnp.int32, (ROWS, LANES), 1)
        for i in range(0, d, CH):
            y[i:i + CH, :] = dot(vwq[c, :, i:i + CH], v, 0, 0).astype(BF16)
        b_norm(y, a, cv, 0, o, y, stats, 0, acc.at[c], 0, ya)
        for i in range(0, d, ROWS):
            e = 0.0
            for k in range(3):
                e = jnp.where(at == 4 + k, token_sum(t[k * d + i:k * d + i + ROWS, :].astype(F32)), e)
            acc[c, i:i + ROWS, :] += e
        then(4)
        then(5)
        for i, v, dst in ((0, dy, dys), (1, u, dgs), (2, o, drs), (3, t, dts)):
            copy(i, v, dst).wait()
        then(2)

    late = 1 - g.side
    loads = [pltpu.make_async_copy(x_in, vwq.at[late, pl.ds(0, tok), :], lead_sems.at[0]),
             pltpu.make_async_copy(dy_in, vwq.at[late, pl.ds(tok, tok), :], lead_sems.at[1]),
             pltpu.make_async_copy(vec, vvec, lead_sems.at[2]), pltpu.make_async_copy(bq, vbq, lead_sems.at[3]),
             pltpu.make_async_copy(b1, vb1, lead_sems.at[4])]
    for cp in loads:
        cp.start()
    for i in range(4):
        weight(g.side, i).start()
    for i in range(1, 4):
        weight(late, i).start()
    barrier = pltpu.get_barrier_semaphore()
    for i in range(n):
        pl.semaphore_signal(barrier, inc=1, device_id={'pp': jnp.int32(i)})
    for cp in loads:
        cp.wait()
    out[0] = vwq[late, 0:tok, :].T
    out[1] = vwq[late, tok:2 * tok, :].T

    @pl.when(g.outside)
    def _():
        slots[0, 0] = out[0]
    fed = [pltpu.make_async_copy(out.at[0], x_t, lead_sems.at[0]), pltpu.make_async_copy(out.at[1], dy_t, lead_sems.at[1])]
    for cp in fed:
        cp.start()
    weight(late, 0).start()
    pl.semaphore_wait(barrier, n)
    for cp in fed:
        cp.wait()

    heads_at = ((0, 0), (1, g.last))
    for k, head in heads_at:
        spot = g.place(g.me + k * (g.last - 2 * g.me))

        @pl.when(g.me != head)
        def _():
            remote(x_t, slots.at[0, spot], feed_send.at[0, k], recv_sems.at[0, 0, spot], jnp.int32(head)).start()
            remote(dy_t, feed.at[spot], feed_send.at[1, k], feed_recv.at[spot], jnp.int32(head)).start()

    for c in range(2):
        rows = [vvec[i, c:c + 1, :] for i in range(6)] + [vbq[c, i:i + 1, :] for i in range(3)]
        rows += [vb1[c:c + 1, i:i + d] for i in range(0, f, d)]
        rows = [v.astype(F32) for v in rows] + [jnp.zeros((LANES - len(rows), d), F32)]
        vcols[c] = jnp.concatenate(rows, 0).T.astype(BF16)
    acc[...] = jnp.zeros_like(acc)

    def settle(par, flag):
        @pl.when(flag == 1)
        def _():
            remote(out.at[par], slots.at[0, 0], send_sems.at[par], recv_sems.at[0, 0, 0], g.me).wait_send()

    def body(s, carry):
        kind, back, sec, m, c = g.step(s)
        nxt = jnp.minimum(s + 1, g.steps - 1)
        _, back2, _, m2, c2 = g.step(nxt)
        more = both(back2, s + 1 < g.steps)
        par = lax.rem(s, 2)
        inward = jnp.logical_or(kind == 0, kind == 2)
        outward = jnp.logical_not(inward)
        way = jnp.where(back, 1, 0)

        @pl.when(jnp.logical_or(s == 0, both(kind == 1, m == 0)))
        def _():
            for i in range(4):
                weight(c, i).wait()

        settle(par, carry[1])

        own = jnp.logical_or(both(outward, g.inside), both(kind == 0, m == 0, g.outside))

        @pl.when(jnp.logical_not(own))
        def _():
            remote(out.at[par], slots.at[sec, m], send_sems.at[par], recv_sems.at[way, sec, m], g.me).wait_recv()

        @pl.when(jnp.logical_not(back))
        def _():
            forward(c, m, slots.at[sec, m], out.at[par])

            @pl.when(more)
            def _():
                for i in (0, 2, 3, 4, 5):
                    fetch(i, c2, m2).start()

        @pl.when(back)
        def _():
            def then(i, at=None):
                @pl.when(more)
                def _():
                    fetch(i, c2, m2, at).start()

            backward(c, m, slots.at[sec, m], out.at[par], then)

        @pl.when(both(inward, g.inside))
        def _():
            slots[1 - sec, m] = out[par]

        @pl.when(both(inward, jnp.logical_not(g.inside)))
        def _():
            remote(out.at[par], slots.at[sec, m], send_sems.at[par], recv_sems.at[way, sec, m], g.inner).start()

        @pl.when(both(outward, jnp.logical_not(g.outside)))
        def _():
            remote(out.at[par], slots.at[sec, m], send_sems.at[par], recv_sems.at[way, sec, m], g.outer).start()

        owner = m + g.side * (g.last - 2 * m)
        done = both(outward, g.outside, m < g.half)
        for w, ref in ((0, y_out), (1, dx_out)):
            mine = both(done, way == w)

            @pl.when(both(mine, owner == g.me))
            def _():
                pltpu.make_async_copy(out.at[par], ref, send_sems.at[par]).start()

            @pl.when(both(mine, owner != g.me))
            def _():
                remote(out.at[par], ref, send_sems.at[par], final_sems.at[w], owner).start()

        @pl.when(both(kind == 1, g.outside))
        def _():
            @pl.when(m == 0)
            def _():
                pltpu.make_async_copy(dy_t, slots.at[1, m], recv_sems.at[1, 1, m]).start()

            @pl.when(m > 0)
            def _():
                remote(dy_t, feed.at[m], feed_send.at[1, 0], feed_recv.at[m], g.me).wait_recv()
                pltpu.make_async_copy(feed.at[m], slots.at[1, m], recv_sems.at[1, 1, m]).start()

        kept = jnp.logical_or(both(inward, g.inside), both(outward, g.outside, m >= g.half))
        return jnp.where(kept, 0, 1), carry[0]

    before, earlier = lax.fori_loop(0, g.steps, body, (jnp.int32(0), jnp.int32(0)))
    settle(g.steps % 2, earlier)
    settle((g.steps + 1) % 2, before)
    for k, head in heads_at:
        @pl.when(g.me != head)
        def _():
            remote(x_t, slots.at[0, 0], feed_send.at[0, k], recv_sems.at[0, 0, 0], jnp.int32(head)).wait_send()
            remote(dy_t, feed.at[0], feed_send.at[1, k], feed_recv.at[0], jnp.int32(head)).wait_send()

    @pl.when(jnp.logical_not(g.outside))
    def _():
        for w, ref in ((0, y_out), (1, dx_out)):
            remote(out.at[0], ref, send_sems.at[0], final_sems.at[w], g.me).wait_recv()

    cp = pltpu.make_async_copy(acc, sums, b_sems.at[0])
    cp.start()
    cp.wait()


def run_walk(n, heads, seq, x, dy, weights, vec, bq, b1):
    tok, d = x.shape
    f = weights[2].shape[2]
    prow = (tok // seq) * (heads // 2) * seq
    st, vm, dma = jax.ShapeDtypeStruct, pltpu.VMEM, pltpu.SemaphoreType.DMA
    act, tall, hid = ((d, tok), BF16), ((3 * d, tok), BF16), ((f, tok), BF16)
    outs = [st(*act)] * 2 + [st((2, n) + v, k) for v, k in (
        act, tall, act, ((prow, 2 * seq), F32), ((2 * f, tok // 2), F32), ((8, tok), F32), act, act, act, hid,
        act, hid, act, tall)] + [st((n, d, tok), BF16), st((2, d, LANES), F32)] + [st(*act)] * 2
    scratch = [vm(w.shape, w.dtype) for w in weights] + [vm((2, d, LANES), BF16)] + [vm(v.shape, v.dtype) for v in (vec, bq, b1)] + [
        vm((2, n, d, tok), BF16), vm((2, d, tok), BF16), vm(*act), vm(*tall), vm(*act), vm(*act), vm(*hid),
        vm((2 * f, tok // 2), F32), vm((d, tok), F32), vm((8, tok), F32), vm((2, d, LANES), F32),
        dma((2, len(weights))), dma((2, 2, n)), dma((2,)), dma((2,)), dma((2, 2)), dma((n,)), dma((10,)), dma((6,)), dma((4,)),
        dma((5,))]
    args = (x, dy, *weights, vec, bq, b1)
    return pl.pallas_call(
        functools.partial(walk_kernel, n, heads, seq), out_shape=outs, in_specs=[HBM] * len(args), out_specs=[HBM] * len(outs),
        scratch_shapes=scratch, name='walk',
        compiler_params=pltpu.CompilerParams(vmem_limit_bytes=VMEM_LIMIT, collective_id=0, has_side_effects=True),
    )(*args)


PAIR = 2


def grads_kernel(n, *refs):
    ins, (y_t, dx_t, sums), refs = refs[:8], refs[8:11], refs[11:]
    outs, (b1_out, y_out, dx_out, vec_out, bq_out), refs = refs[:4], refs[4:9], refs[9:]
    accs, biases, refs = refs[:4], refs[4:7], refs[7:]
    buf, va, vb, vsum, b1_row, vec_rows, bq_rows, in_sems, out_sems, end_sems = refs
    steps = n // PAIR
    tok = buf.shape[3]
    d = y_t.shape[0]

    def fetches(c, k, j):
        slot = lax.rem(j, 2)
        rows, cols = ins[2 * k].shape[2], ins[2 * k + 1].shape[2]
        at = pl.ds(j * PAIR, PAIR)
        return (pltpu.make_async_copy(ins[2 * k].at[c, at], buf.at[slot, :, pl.ds(0, rows), :], in_sems.at[slot, 0]),
                pltpu.make_async_copy(ins[2 * k + 1].at[c, at], buf.at[slot, :, pl.ds(rows, cols), :], in_sems.at[slot, 1]))

    def begin(c, k, j):
        for cp in fetches(c, k, j):
            cp.start()

    def results(c, k):
        cps = [pltpu.make_async_copy(accs[k], outs[k].at[c], out_sems.at[k])]
        return cps

    begin(jnp.int32(0), 0, jnp.int32(0))
    acts = ((y_t, y_out), (dx_t, dx_out))
    loads = [pltpu.make_async_copy(h, va.at[i], end_sems.at[i]) for i, (h, _) in enumerate(acts)]
    loads.append(pltpu.make_async_copy(sums, vsum, end_sems.at[2]))
    for cp in loads:
        cp.start()
    for cp in loads:
        cp.wait()
    for i in range(2):
        vb[i] = va[i].T
    turned = [pltpu.make_async_copy(vb.at[i], h, end_sems.at[i]) for i, (_, h) in enumerate(acts)]
    for cp in turned:
        cp.start()
    for i in range(2):
        part = vsum[i].T
        for row, src in ((0, 0), (1, 1), (3, 2), (4, 3)):
            vec_rows[i, row] = part[src:src + 1, :]
        for row in range(3):
            bq_rows[i, row] = part[4 + row:5 + row, :]

    def stage(c, carry):
        for k in range(4):
            rows, cols = ins[2 * k].shape[2], ins[2 * k + 1].shape[2]

            def step(j, carry, k=k, rows=rows, cols=cols):
                @pl.when(j + 1 < steps)
                def _():
                    begin(c, k, j + 1)

                @pl.when(j + 1 == steps)
                def _():
                    if k < 3:
                        begin(c, k + 1, jnp.int32(0))
                    else:
                        @pl.when(c == 0)
                        def _():
                            begin(jnp.int32(1), 0, jnp.int32(0))

                @pl.when(jnp.logical_and(j == 0, c == 1))
                def _():
                    for cp in results(jnp.int32(0), k):
                        cp.wait()

                for cp in fetches(c, k, j):
                    cp.wait()
                slot = lax.rem(j, 2)
                later = j > 0
                parts = 2 if max(rows, cols) > 3 * d else 1
                tall = rows > cols
                height, width = (rows // parts, cols) if tall else (rows, cols // parts)

                def block(h, carry):
                    top = pl.multiple_of(h * height, CH) if tall and parts > 1 else 0
                    left = pl.multiple_of(h * width, CH) if not tall and parts > 1 else 0
                    w = [buf[slot, q, pl.ds(rows + left, width), :] for q in range(PAIR)]
                    for i in range(0, height, CH):
                        at = (pl.ds(top + i, CH), pl.ds(left, width))
                        z = jnp.where(later, accs[k][at], 0.0)
                        edge = i == 0 and k < 3
                        if edge:
                            e = jnp.where(later, biases[k][:, at[1]], 0.0)
                        for q in range(PAIR):
                            x = buf[slot, q, pl.ds(top + i, CH), :]
                            if edge:
                                x = jnp.concatenate([x, jnp.ones((16, tok), BF16)], 0)
                            v = rounded(dot(x, w[q], 1, 1))
                            z = z + v[:CH]
                            if edge:
                                e = e + v[CH:CH + 8]
                        accs[k][at] = z
                        if edge and tall and parts > 1:
                            biases[k][:, at[1]] = jnp.where(h == 0, e, biases[k][:, at[1]])
                        elif edge:
                            biases[k][:, at[1]] = e
                    return carry

                if parts > 1:
                    lax.fori_loop(0, parts, block, 0)
                else:
                    block(0, 0)
                return carry

            lax.fori_loop(0, steps, step, 0)
            for cp in results(c, k):
                cp.start()
        b1_row[c] = biases[0][0:1, :]
        vec_rows[c, 5] = biases[1][0:1, :]
        vec_rows[c, 2] = biases[2][0:1, :]
        return carry

    lax.fori_loop(0, 2, stage, 0)
    rows = [pltpu.make_async_copy(v, h, end_sems.at[2 + i])
            for i, (v, h) in enumerate(((b1_row, b1_out), (vec_rows, vec_out), (bq_rows, bq_out)))]
    for cp in rows:
        cp.start()
    for cp in rows + turned:
        cp.wait()
    for k in range(4):
        for cp in results(jnp.int32(1), k):
            cp.wait()


def run_grads(pairs, y_t, dx_t, sums):
    n, tok = pairs[0][0].shape[1], pairs[0][0].shape[3]
    sizes = [(a.shape[2], b.shape[2]) for a, b in pairs]
    d, f = sizes[0]
    st, vm, dma = jax.ShapeDtypeStruct, pltpu.VMEM, pltpu.SemaphoreType.DMA
    most = max(a + b for a, b in sizes)
    rows = [((2, 1, f), F32), ((2, 6, 1, d), F32), ((2, 3, 1, d), F32)]
    return pl.pallas_call(
        functools.partial(grads_kernel, n),
        out_shape=[st((2,) + v, F32) for v in sizes] + [st(*rows[0]), st((tok, d), BF16), st((tok, d), BF16), st(*rows[1]),
                                                        st(*rows[2])],
        in_specs=[HBM] * 11, out_specs=[HBM] * 9,
        scratch_shapes=[vm(v, F32) for v in sizes] + [vm((8, v[1]), F32) for v in sizes[:3]] + [
            vm((2, PAIR, most, tok), BF16), vm((2, d, tok), BF16), vm((2, tok, d), BF16), vm(sums.shape, F32)] + [
            vm(*v) for v in rows] + [dma((2, 2)), dma((4,)), dma((5,))],
        name='weight_grads', compiler_params=pltpu.CompilerParams(vmem_limit_bytes=VMEM_LIMIT),
    )(*[v for p in pairs for v in p], y_t, dx_t, sums)


def solution(mesh):
    data_spec = P(('dp', 'pp'))
    weight_spec = P('pp')

    def per_device(x, dy, w_qkv, w_attn, w_fc, w_proj, b_qkv, b_fc, vec_d):
        _, batch, seq, d = x.shape
        heads = w_qkv.shape[5]
        tok = batch * seq

        weights = (w_qkv.reshape(2, d, 3 * d).transpose(0, 2, 1), w_attn.reshape(2, d, d), w_fc[0, :, 0], w_proj[0, :, 0])
        y_t, dx_t, *stash = run_walk(
            mesh.shape['pp'], heads, seq, x.reshape(tok, d), dy.reshape(tok, d), weights,
            vec_d[0, :, 0].transpose(1, 0, 2), b_qkv.reshape(2, 3, d), b_fc[0, :, 0])
        as_, os_, bs, us, dys, dgs, drs, dts, _, sums = stash[6:16]
        g1, g2, go, gq, gb1, y, dx, gv, gbq = run_grads(((bs, dgs), (us, dys), (os_, drs), (dts, as_)), y_t, dx_t, sums)
        return (y.reshape(x.shape), dx.reshape(x.shape),
                gq.transpose(0, 2, 1).reshape(w_qkv.shape), go.reshape(w_attn.shape), g1.reshape(w_fc.shape),
                g2.reshape(w_proj.shape), gbq.reshape(b_qkv.shape), gb1.reshape(b_fc.shape), gv.reshape(vec_d.shape))

    return jax.shard_map(per_device, mesh=mesh, in_specs=(data_spec, data_spec) + (weight_spec,) * 7,
                         out_specs=(data_spec, data_spec) + (data_spec,) * 7, check_vma=False)
```

profile of v0, /device:TPU:127, one launch (start us, length us, event | category | flops | bytes accessed | tf_op | source)
XLA Modules:
  0.0 703.8 jit_solution(3662742082049957515)
XLA Ops:
  0.6 1.4 reshape.74.bq
  2.1 548.6 %walk.1 = (bf16[768,512]{1,0:T(8,128)(2,1)}, bf16[768,512]{1,0:T(8,128)(2,1)}, bf16[2,8,768,512]{3,2,1,0:T(8,128)(2,1)}, bf16[2,8,2304,512]{3,2,1,0:T(8,128)(2,1...) custom-call(bf16[512,768]{1,0:T(8,128)(2,1)} %bitcast.39, ...), custom_call_target="tpu_custom_call" | custom-call | tf_op jit(solution)/shard_map/walk/pallas_call | solution.py:526
  550.7 151.6 %weight_grads.1 = (f32[2,768,3072]{2,1,0:T(8,128)}, f32[2,3072,768]{2,1,0:T(8,128)}, f32[2,768,768]{2,1,0:T(8,128)}, f32[2,2304,768]{2,1,0:T(8,128)}, f32[2,1,30...) custom-call(bf16[2,8,768,512]{3,2,1,0:T(8,128)(2,1)} %get-tuple-elem, ...), custom_call_target="tpu_custom_call" | custom-call | tf_op jit(solution)/shard_map/weight_grads/pallas_call | solution.py:669
  702.3 0.8 reduce
  703.1 0.7 reshape.71
where the time goes:
time: 704 us
  Pallas kernels  700 us (99%)
    pallas_call x1, Pallas kernels, run_walk(): pl.pallas_call(functools.partial(walk_kernel, n, heads, seq), out_shape=o...  549 us
    pallas_call x1, Pallas kernels, run_grads(): pl.pallas_call(functools.partial(grads_kernel, n), out_shape=[st((2,) + v...  152 us

commit v1 on v0

--- a/solution.py
+++ b/solution.py
@@ -13,6 +13,7 @@
 LANES = 128
 ROWS = 96
 CH = 256
+GROUP = 256
 SKEW = 8
 K0 = 0.7978845608028654
 K1 = K0 * 0.044715
@@ -50,11 +51,12 @@
     return jnp.concatenate([jnp.concatenate([a, z], 1), jnp.concatenate([z, b], 1)], 0)
 
 
-def f_norm(src, cols, lane, dst, stats, row, hold):
+def f_norm(src, cols, lane, dst, stats, row, hold, acc=None):
     d, t = src.shape
-    acc = jnp.zeros((8, t), F32)
-    for i in range(0, d, ROWS):
-        acc += rows_sum(src[i:i + ROWS, :].astype(F32))
+    if acc is None:
+        acc = jnp.zeros((8, t), F32)
+        for i in range(0, d, ROWS):
+            acc += rows_sum(src[i:i + ROWS, :].astype(F32))
     mean = jnp.sum(acc, axis=0, keepdims=True) * (1.0 / d)
     acc = jnp.zeros((8, t), F32)
     for i in range(0, d, ROWS):
@@ -274,20 +276,23 @@
         f_heads(t, o, pg, heads, seq, lambda b: copy(4, pg, ps, (b * part, part)).start())
         copy(3, o, os_).start()
         v = o[...]
+        total = jnp.zeros((8, tok), F32)
         for i in range(0, d, CH):
             z = dot(vwo[c, :, i:i + CH], v, 0, 0) + column(cv, 2, i, CH) + x[i:i + CH, :].astype(F32)
-            r[i:i + CH, :] = z.astype(BF16)
+            z = z.astype(BF16)
+            r[i:i + CH, :] = z
+            total += rows_sum(z.astype(F32))
         copy(5, r, rs).start()
         copy(1, a, as_).wait()
-        f_norm(r, cv, 3, a, stats, 2, ya)
+        f_norm(r, cv, 3, a, stats, 2, ya, total)
         copy(6, a, bs).start()
         copy(7, stats, ss).start()
         copy(4, pg.at[pl.ds(0, prow), :], ps).wait()
         v = a[...]
 
         def up(k):
-            for i in range(k * d, (k + 1) * d, CH):
-                h = dot(vw1[c, :, i:i + CH], v, 0, 0) + column(cv, 9 + k, i % d, CH)
+            for i in range(k * GROUP, (k + 1) * GROUP, CH):
+                h = dot(vw1[c, :, i:i + CH], v, 0, 0) + column(cv, 9 + i // d, i % d, CH)
                 uu, slope = gelu_and_slope(h)
                 u[i:i + CH, :] = uu.astype(BF16)
                 pg[2 * i:2 * i + CH, :] = slope[:, :half]
@@ -296,20 +301,22 @@
                 copy(9, pg, gs, (2 * i, 2 * CH)).start()
 
         def down(k):
-            w = u[k * d:(k + 1) * d, :]
+            ks = slice(k * GROUP, (k + 1) * GROUP)
+            w = u[ks, :]
             for i in range(0, d, CH):
-                z = dot(vw2[c, k * d:(k + 1) * d, i:i + CH], w, 0, 0)
+                z = dot(vw2[c, ks, i:i + CH], w, 0, 0)
                 z += (column(cv, 5, i, CH) + r[i:i + CH, :].astype(F32)) if k == 0 else ya[i:i + CH, :]
-                if (k + 1) * d < f:
+                if ks.stop < f:
                     ya[i:i + CH, :] = z
                 else:
                     y[i:i + CH, :] = z.astype(BF16)
 
-        up(0)
-        for k in range(1, f // d):
-            up(k)
-            down(k - 1)
-        down(f // d - 1)
+        many = f // GROUP
+        for k in range(many + 2):
+            if k < many:
+                up(k)
+            if k >= 2:
+                down(k - 2)
         for i, v, dst in ((0, x, hs), (2, t, ts), (3, o, os_), (5, r, rs), (6, a, bs), (7, stats, ss), (8, u, us),
                           (9, pg, gs)):
             copy(i, v, dst).wait()
@@ -367,8 +374,6 @@
         cp.start()
     for i in range(4):
         weight(g.side, i).start()
-    for i in range(1, 4):
-        weight(late, i).start()
     barrier = pltpu.get_barrier_semaphore()
     for i in range(n):
         pl.semaphore_signal(barrier, inc=1, device_id={'pp': jnp.int32(i)})
@@ -383,7 +388,6 @@
     fed = [pltpu.make_async_copy(out.at[0], x_t, lead_sems.at[0]), pltpu.make_async_copy(out.at[1], dy_t, lead_sems.at[1])]
     for cp in fed:
         cp.start()
-    weight(late, 0).start()
     pl.semaphore_wait(barrier, n)
     for cp in fed:
         cp.wait()
@@ -423,6 +427,11 @@
         def _():
             for i in range(4):
                 weight(c, i).wait()
+
+        @pl.when(s == 0)
+        def _():
+            for i in range(4):
+                weight(late, i).start()
 
         settle(par, carry[1])
 
@@ -557,12 +566,12 @@
         cps = [pltpu.make_async_copy(accs[k], outs[k].at[c], out_sems.at[k])]
         return cps
 
-    begin(jnp.int32(0), 0, jnp.int32(0))
     acts = ((y_t, y_out), (dx_t, dx_out))
     loads = [pltpu.make_async_copy(h, va.at[i], end_sems.at[i]) for i, (h, _) in enumerate(acts)]
     loads.append(pltpu.make_async_copy(sums, vsum, end_sems.at[2]))
     for cp in loads:
         cp.start()
+    begin(jnp.int32(0), 0, jnp.int32(0))
     for cp in loads:
         cp.wait()
     for i in range(2):
@@ -615,9 +624,9 @@
                     for i in range(0, height, CH):
                         at = (pl.ds(top + i, CH), pl.ds(left, width))
                         z = jnp.where(later, accs[k][at], 0.0)
-                        edge = i == 0 and k < 3
+                        edge = i == 0 and k > 0
                         if edge:
-                            e = jnp.where(later, biases[k][:, at[1]], 0.0)
+                            e = jnp.where(later, biases[k - 1][:, at[1]], 0.0)
                         for q in range(PAIR):
                             x = buf[slot, q, pl.ds(top + i, CH), :]
                             if edge:
@@ -628,9 +637,9 @@
                                 e = e + v[CH:CH + 8]
                         accs[k][at] = z
                         if edge and tall and parts > 1:
-                            biases[k][:, at[1]] = jnp.where(h == 0, e, biases[k][:, at[1]])
+                            biases[k - 1][:, at[1]] = jnp.where(h == 0, e, biases[k - 1][:, at[1]])
                         elif edge:
-                            biases[k][:, at[1]] = e
+                            biases[k - 1][:, at[1]] = e
                     return carry
 
                 if parts > 1:
@@ -662,7 +671,7 @@
 def run_grads(pairs, y_t, dx_t, sums):
     n, tok = pairs[0][0].shape[1], pairs[0][0].shape[3]
     sizes = [(a.shape[2], b.shape[2]) for a, b in pairs]
-    d, f = sizes[0]
+    d, f = sizes[1]
     st, vm, dma = jax.ShapeDtypeStruct, pltpu.VMEM, pltpu.SemaphoreType.DMA
     most = max(a + b for a, b in sizes)
     rows = [((2, 1, f), F32), ((2, 6, 1, d), F32), ((2, 3, 1, d), F32)]
@@ -671,7 +680,7 @@
         out_shape=[st((2,) + v, F32) for v in sizes] + [st(*rows[0]), st((tok, d), BF16), st((tok, d), BF16), st(*rows[1]),
                                                         st(*rows[2])],
         in_specs=[HBM] * 11, out_specs=[HBM] * 9,
-        scratch_shapes=[vm(v, F32) for v in sizes] + [vm((8, v[1]), F32) for v in sizes[:3]] + [
+        scratch_shapes=[vm(v, F32) for v in sizes] + [vm((8, v[1]), F32) for v in sizes[1:]] + [
             vm((2, PAIR, most, tok), BF16), vm((2, d, tok), BF16), vm((2, tok, d), BF16), vm(sums.shape, F32)] + [
             vm(*v) for v in rows] + [dma((2, 2)), dma((4,)), dma((5,))],
         name='weight_grads', compiler_params=pltpu.CompilerParams(vmem_limit_bytes=VMEM_LIMIT),
@@ -692,7 +701,7 @@
             mesh.shape['pp'], heads, seq, x.reshape(tok, d), dy.reshape(tok, d), weights,
             vec_d[0, :, 0].transpose(1, 0, 2), b_qkv.reshape(2, 3, d), b_fc[0, :, 0])
         as_, os_, bs, us, dys, dgs, drs, dts, _, sums = stash[6:16]
-        g1, g2, go, gq, gb1, y, dx, gv, gbq = run_grads(((bs, dgs), (us, dys), (os_, drs), (dts, as_)), y_t, dx_t, sums)
+        gq, g1, g2, go, gb1, y, dx, gv, gbq = run_grads(((dts, as_), (bs, dgs), (us, dys), (os_, drs)), y_t, dx_t, sums)
         return (y.reshape(x.shape), dx.reshape(x.shape),
                 gq.transpose(0, 2, 1).reshape(w_qkv.shape), go.reshape(w_attn.shape), g1.reshape(w_fc.shape),
                 g2.reshape(w_proj.shape), gbq.reshape(b_qkv.shape), gb1.reshape(b_fc.shape), gv.reshape(vec_d.shape))

time: 704 us -> 698 us (level)
  no operation moved by 1% of the time
where the time goes in v1:
time: 698 us
  Pallas kernels  694 us (99%)
    pallas_call x1, Pallas kernels, run_walk(): pl.pallas_call(functools.partial(walk_kernel, n, heads, seq), out_shape=o...  547 us
    pallas_call x1, Pallas kernels, run_grads(): pl.pallas_call(functools.partial(grads_kernel, n), out_shape=[st((2,) + v...  147 us

profile of v1, /device:TPU:127, one launch (start us, length us, event | category | flops | bytes accessed | tf_op | source)
XLA Modules:
  0.0 698.0 jit_solution(4392326628504977536)
XLA Ops:
  0.6 1.4 reshape.74.bq
  2.1 547.2 %walk.1 = (bf16[768,512]{1,0:T(8,128)(2,1)}, bf16[768,512]{1,0:T(8,128)(2,1)}, bf16[2,8,768,512]{3,2,1,0:T(8,128)(2,1)}, bf16[2,8,2304,512]{3,2,1,0:T(8,128)(2,1...) custom-call(bf16[512,768]{1,0:T(8,128)(2,1)} %bitcast.39, ...), custom_call_target="tpu_custom_call" | custom-call | tf_op jit(solution)/shard_map/walk/pallas_call | solution.py:535
  549.3 147.2 %weight_grads.1 = (f32[2,2304,768]{2,1,0:T(8,128)}, f32[2,768,3072]{2,1,0:T(8,128)}, f32[2,3072,768]{2,1,0:T(8,128)}, f32[2,768,768]{2,1,0:T(8,128)}, f32[2,1,30...) custom-call(bf16[2,8,2304,512]{3,2,1,0:T(8,128)(2,1)} %get-tuple-ele, ...), custom_call_target="tpu_custom_call" | custom-call | tf_op jit(solution)/shard_map/weight_grads/pallas_call | solution.py:678
  696.5 0.8 reduce
  697.3 0.7 reshape.71

commit v2 on v1

--- a/solution.py
+++ b/solution.py
@@ -262,9 +262,14 @@
             hbm, v = hbm.at[pl.ds(*at), :], v.at[pl.ds(*at), :]
         return pltpu.make_async_copy(hbm, v, b_in.at[i])
 
-    def forward(c, m, x, y):
+    def forward(c, m, x, y, pending, more_forward):
         copy = saver(c, m, f_sems)
         cv = vcols.at[c]
+
+        def tail():
+            copy(8, u, us).wait()
+            copy(10, pg, gs, (prow, 2 * f - prow)).wait()
+
         copy(0, x, hs).start()
         f_norm(x, cv, 0, a, stats, 0, ya)
         copy(1, a, as_).start()
@@ -288,6 +293,11 @@
         copy(6, a, bs).start()
         copy(7, stats, ss).start()
         copy(4, pg.at[pl.ds(0, prow), :], ps).wait()
+
+        @pl.when(pending)
+        def _():
+            tail()
+
         v = a[...]
 
         def up(k):
@@ -298,7 +308,7 @@
                 pg[2 * i:2 * i + CH, :] = slope[:, :half]
                 pg[2 * i + CH:2 * i + 2 * CH, :] = slope[:, half:]
                 copy(8, u, us, (i, CH)).start()
-                copy(9, pg, gs, (2 * i, 2 * CH)).start()
+                copy(9 if 2 * i < prow else 10, pg, gs, (2 * i, 2 * CH)).start()
 
         def down(k):
             ks = slice(k * GROUP, (k + 1) * GROUP)
@@ -317,9 +327,13 @@
                 up(k)
             if k >= 2:
                 down(k - 2)
-        for i, v, dst in ((0, x, hs), (2, t, ts), (3, o, os_), (5, r, rs), (6, a, bs), (7, stats, ss), (8, u, us),
-                          (9, pg, gs)):
+        for i, v, dst in ((0, x, hs), (2, t, ts), (3, o, os_), (5, r, rs), (6, a, bs), (7, stats, ss)):
             copy(i, v, dst).wait()
+        copy(9, pg, gs, (0, prow)).wait()
+
+        @pl.when(jnp.logical_not(more_forward))
+        def _():
+            tail()
 
     def backward(c, m, dy, y, then):
         copy = saver(c, m, b_sems)
@@ -416,8 +430,9 @@
     def body(s, carry):
         kind, back, sec, m, c = g.step(s)
         nxt = jnp.minimum(s + 1, g.steps - 1)
-        _, back2, _, m2, c2 = g.step(nxt)
+        kind2, back2, _, m2, c2 = g.step(nxt)
         more = both(back2, s + 1 < g.steps)
+        onward = both(kind < 2, kind2 < 2)
         par = lax.rem(s, 2)
         inward = jnp.logical_or(kind == 0, kind == 2)
         outward = jnp.logical_not(inward)
@@ -443,7 +458,7 @@
 
         @pl.when(jnp.logical_not(back))
         def _():
-            forward(c, m, slots.at[sec, m], out.at[par])
+            forward(c, m, slots.at[sec, m], out.at[par], carry[2] == 1, onward)
 
             @pl.when(more)
             def _():
@@ -496,9 +511,9 @@
                 pltpu.make_async_copy(feed.at[m], slots.at[1, m], recv_sems.at[1, 1, m]).start()
 
         kept = jnp.logical_or(both(inward, g.inside), both(outward, g.outside, m >= g.half))
-        return jnp.where(kept, 0, 1), carry[0]
-
-    before, earlier = lax.fori_loop(0, g.steps, body, (jnp.int32(0), jnp.int32(0)))
+        return jnp.where(kept, 0, 1), carry[0], jnp.where(onward, 1, 0)
+
+    before, earlier, _ = lax.fori_loop(0, g.steps, body, (jnp.int32(0),) * 3)
     settle(g.steps % 2, earlier)
     settle((g.steps + 1) % 2, before)
     for k, head in heads_at:
@@ -529,7 +544,7 @@
     scratch = [vm(w.shape, w.dtype) for w in weights] + [vm((2, d, LANES), BF16)] + [vm(v.shape, v.dtype) for v in (vec, bq, b1)] + [
         vm((2, n, d, tok), BF16), vm((2, d, tok), BF16), vm(*act), vm(*tall), vm(*act), vm(*act), vm(*hid),
         vm((2 * f, tok // 2), F32), vm((d, tok), F32), vm((8, tok), F32), vm((2, d, LANES), F32),
-        dma((2, len(weights))), dma((2, 2, n)), dma((2,)), dma((2,)), dma((2, 2)), dma((n,)), dma((10,)), dma((6,)), dma((4,)),
+        dma((2, len(weights))), dma((2, 2, n)), dma((2,)), dma((2,)), dma((2, 2)), dma((n,)), dma((11,)), dma((6,)), dma((4,)),
         dma((5,))]
     args = (x, dy, *weights, vec, bq, b1)
     return pl.pallas_call(

time: 698 us -> 693 us (level)
  no operation moved by 1% of the time
where the time goes in v2:
time: 693 us
  Pallas kernels  689 us (99%)
    pallas_call x1, Pallas kernels, run_walk(): pl.pallas_call(functools.partial(walk_kernel, n, heads, seq), out_shape=o...  542 us
    pallas_call x1, Pallas kernels, run_grads(): pl.pallas_call(functools.partial(grads_kernel, n), out_shape=[st((2,) + v...  147 us

profile of v2, /device:TPU:127, one launch (start us, length us, event | category | flops | bytes accessed | tf_op | source)
XLA Modules:
  0.0 692.7 jit_solution(17297339732388201860)
XLA Ops:
  0.6 1.4 reshape.74.bq
  2.1 541.9 %walk.1 = (bf16[768,512]{1,0:T(8,128)(2,1)}, bf16[768,512]{1,0:T(8,128)(2,1)}, bf16[2,8,768,512]{3,2,1,0:T(8,128)(2,1)}, bf16[2,8,2304,512]{3,2,1,0:T(8,128)(2,1...) custom-call(bf16[512,768]{1,0:T(8,128)(2,1)} %bitcast.39, ...), custom_call_target="tpu_custom_call" | custom-call | tf_op jit(solution)/shard_map/walk/pallas_call | solution.py:550
  544.0 147.2 %weight_grads.1 = (f32[2,2304,768]{2,1,0:T(8,128)}, f32[2,768,3072]{2,1,0:T(8,128)}, f32[2,3072,768]{2,1,0:T(8,128)}, f32[2,768,768]{2,1,0:T(8,128)}, f32[2,1,30...) custom-call(bf16[2,8,2304,512]{3,2,1,0:T(8,128)(2,1)} %get-tuple-ele, ...), custom_call_target="tpu_custom_call" | custom-call | tf_op jit(solution)/shard_map/weight_grads/pallas_call | solution.py:693
  691.2 0.8 reduce
  692.0 0.7 reshape.71
